TPU v7x, 32 devices: a whole 2x2x4 slice. The times are simulated.
32 devices in a mesh: grp: 2 (over core), ex: 16 (over z, y, x).
Axes of the slice: x: 2, y: 2, z: 4, core: 2. Of those that a mesh axis runs over, the one named last changes fastest.
Arguments:
- tokens: bfloat16 [8192, 1024], P(('grp', 'ex')), may hold values from -6 to 6
- expert_ids: int32 [8192], P(('grp', 'ex')), may hold values from 0 to 15, as said below
- slot_ids: int32 [8192], P(('grp', 'ex')), may hold values from 0 to 31, as said below
- centroids: bfloat16 [16, 1024], replicated, may hold values from -0.1875 to 0.1875
- w_in: bfloat16 [16, 1024, 4096], P('ex', None, 'grp'), may hold values from -0.1875 to 0.1875
- w_out: bfloat16 [16, 4096, 1024], P('ex', 'grp'), may hold values from -0.09375 to 0.09375
Outputs:
- combined: bfloat16 [8192, 1024], P(('grp', 'ex'))
Inputs may be any that keep to these rules, and one draw needn't show every extreme that they name: `expert_ids`: within each device's 256 rows, at most 32 rows name one expert; in every device some expert is named by exactly 32 rows, and in each group of 16 devices along ex one expert is named by 32 rows on every device of the group. `slot_ids`: rows of one device that name the same expert have distinct slots.
All inputs are finite; a program needn't handle non-finite values.
Results may differ from a plain program's by a relative error of at most 0.0035.
Values may be sent and summed in bfloat16 or wider, within the bound.
A program may use at most 128 MiB of HBM per device.

v0:
```python
import jax
import jax.numpy as jnp
from jax import lax
from jax.sharding import PartitionSpec as P


def on_device(tokens, expert_ids, slot_ids, centroids, w_in, w_out):
    experts = centroids.shape[0]
    count_rows = tokens.shape[0]
    model_width = tokens.shape[1]
    capacity = 2 * count_rows // experts
    buffer_rows = expert_ids * capacity + slot_ids
    outgoing = (
        jnp.zeros((experts * capacity, model_width), jnp.bfloat16).at[buffer_rows].set(tokens)
    )
    outgoing = outgoing.reshape(experts, capacity, model_width)
    scores = jnp.dot(tokens, centroids.T, preferred_element_type=jnp.float32)
    columns = jnp.arange(experts, dtype=jnp.int32)
    chosen = jnp.sum(jnp.where(columns[None, :] == expert_ids[:, None], scores, 0.0), axis=1)
    gating = jax.nn.sigmoid(chosen)
    full_in, full_out = (
        lax.all_gather(w_in, "grp", axis=2, tiled=True),
        lax.all_gather(w_out, "grp", axis=1, tiled=True),
    )
    received = lax.all_to_all(outgoing, "ex", split_axis=0, concat_axis=0, tiled=True)
    flat_rows = received.reshape(-1, model_width)
    hidden = jnp.maximum(
        jnp.dot(flat_rows, full_in[0], preferred_element_type=jnp.float32), 0.0
    ).astype(jnp.bfloat16)
    result = jnp.dot(hidden, full_out[0], preferred_element_type=jnp.float32)
    returned = lax.all_to_all(
        result.astype(jnp.bfloat16).reshape(received.shape),
        "ex",
        split_axis=0,
        concat_axis=0,
        tiled=True,
    )
    arrived = returned.reshape(-1, model_width)[buffer_rows]
    mixed_rows = tokens.astype(jnp.float32) + gating[:, None] * arrived.astype(jnp.float32)
    return mixed_rows.astype(jnp.bfloat16)


def solution(mesh):
    in_specs = (
        P(("grp", "ex"), None),
        P(("grp", "ex")),
        P(("grp", "ex")),
        P(),
        P("ex", None, "grp"),
        P("ex", "grp", None),
    )
    out_specs = P(("grp", "ex"), None)
    return jax.shard_map(
        on_device, mesh=mesh, in_specs=in_specs, out_specs=out_specs, check_vma=False
    )
```

profile of v0, /device:TPU:0, one launch (start us, length us, event | category | flops | bytes accessed | tf_op | source)
XLA Modules:
  0.0 110.2 jit_solution(7864859476668906878)
XLA Ops:
  6.5 0.0 copy-start
  6.5 0.0 copy-start.2
  6.5 0.0 copy-start.3
  6.5 0.0 copy-start.1
  6.5 0.0 all-gather.3.cloned.1.call-start
  6.6 0.7 all-gather.3.cloned.1.call-update
  7.3 0.0 all-gather.5.cloned.1.call-start
  7.3 0.7 all-gather.5.cloned.1.call-update
  8.0 0.0 copy-done.2
  8.0 0.0 copy-done.3
  8.1 0.0 copy-done.1
  8.1 1.9 %scatter_custom_fusion = bf16[512,1024]{1,0:T(8,128)(2,1)S(1)} fusion(s32[256]{0:T(256)S(1)} %compare_select_fusion, bf16[256,1024]{1,0:T(8,128)(2,1)S(1)} %copy-done.1, bf16[]{:T(256)} %constant.1.clone.1), kind=kCustom, calls=%fused_computation.12 | custom fusion | bytes 1048578 | tf_op jit(solution)/shard_map/scatter | solution.py:14
  10.0 34.5 %all_to_all.10 = bf16[16,32,1024]{2,1,0:T(8,128)(2,1)S(1)} all-to-all(bf16[16,32,1024]{2,1,0:T(8,128)(2,1)S(1)} %bitcast.22), channel_id=1, replica_groups=mesh['grp'=2,'ex'=16] {'ex'}, dimensions={0} | all-to-all | bytes 2097152 | tf_op jit(solution)/shard_map/all_to_all | solution.py:25
  44.4 0.0 all-gather.3.cloned.1.call-done
  44.4 9.6 %all-gather.5.cloned.1.call-done = bf16[1,4096,1024]{2,1,0:T(8,128)(2,1)} async-done(((bf16[1,2048,1024]{2,1,0:T(8,128)(2,1)}), bf16[1,4096,1024]{2,1,0:T(8,128)(2,1)}) %all-gather.5.cloned.1.call-update) | async-done | bytes 8388624 | tf_op jit(solution)/shard_map/all_gather | solution.py:23
  54.1 15.6 %fusion.9 = bf16[512,1024]{1,0:T(8,128)(2,1)} fusion(bf16[1,4096,1024]{2,1,0:T(8,128)(2,1)} %all-gather.5.cloned.1.call-done, bf16[512,1024]{1,0:T(8,128)(2,1)S(1)} %bitcast.23, bf16[1,1024,4096]{2,1,0:T(8,128)(2,1)} %all-gather.3.cloned.1.call-done), kind=kOutput, calls=%fused_computation.8 | convolution fusion | flops 8594653184 | bytes 18874368 | tf_op jit(solution)/shard_map/dot_general | solution.py:30
  69.7 6.8 %all-to-all-start.1 = ((bf16[16,32,1024]{2,1,0:T(8,128)(2,1)}), bf16[16,32,1024]{2,1,0:T(8,128)(2,1)S(1)}, u32[]{:S(2)}, u32[]{:S(2)}) async-start(bf16[16,32,1024]{2,1,0:T(8,128)(2,1)} %bitcast.4), calls=%async_computation.1 | async-start | bytes 2097152 | tf_op jit(solution)/shard_map/all_to_all | solution.py:31
  76.5 0.0 copy-done
  76.5 0.3 fusion.14
  76.8 24.4 %all-to-all-done.1 = bf16[16,32,1024]{2,1,0:T(8,128)(2,1)S(1)} async-done(((bf16[16,32,1024]{2,1,0:T(8,128)(2,1)}), bf16[16,32,1024]{2,1,0:T(8,128)(2,1)S(1)}, u32[]{:S(2)}, u32[]{:S(2)}) %all-to-all-start.1) | async-done | bytes 1048608 | tf_op jit(solution)/shard_map/all_to_all | solution.py:31
  101.1 1.2 %gather_fusion = bf16[256,1024]{1,0:T(8,128)(2,1)S(1)} fusion(bf16[512,1024]{1,0:T(8,128)(2,1)S(1)} %bitcast.21, s32[1024]{0:T(1024)S(1)} %pad_clamp_fusion), kind=kCustom, calls=%fused_computation | custom fusion | bytes 1049600 | tf_op jit(solution)/shard_map/gather | solution.py:38
  102.3 1.0 add_convert_fusion
  (3 shorter events, 0.0 us)
Async XLA Ops:
  6.5 69.9 %copy-start = (bf16[16,1024]{1,0:T(8,128)(2,1)S(1)}, bf16[16,1024]{1,0:T(8,128)(2,1)}, u32[]{:S(2)}) copy-start(bf16[16,1024]{1,0:T(8,128)(2,1)} %param.9) | copy-start | bytes 98308
  6.5 1.5 %copy-start.2 = (s32[256]{0:T(256)S(1)}, s32[256]{0:T(256)}, u32[]{:S(2)}) copy-start(s32[256]{0:T(256)} %param.7) | copy-start | bytes 3076
  6.5 1.5 %copy-start.3 = (s32[256]{0:T(256)S(1)}, s32[256]{0:T(256)}, u32[]{:S(2)}) copy-start(s32[256]{0:T(256)} %param.8) | copy-start | bytes 3076
  6.5 1.5 %copy-start.1 = (bf16[256,1024]{1,0:T(8,128)(2,1)S(1)}, bf16[256,1024]{1,0:T(8,128)(2,1)}, u32[]{:S(2)}) copy-start(bf16[256,1024]{1,0:T(8,128)(2,1)} %param.6) | copy-start | bytes 1572868
  6.5 37.9 %all-gather.3.cloned.1.call-start = ((), (), s32[]{:S(2)}) async-start(), calls=%async_computation.2 | async-start | bytes 12582912 | tf_op jit(solution)/shard_map/all_gather | solution.py:22
  7.3 46.8 %all-gather.5.cloned.1.call-start = ((), (), s32[]{:S(2)}) async-start(), calls=%async_computation.3 | async-start | bytes 12582912 | tf_op jit(solution)/shard_map/all_gather | solution.py:23
  69.7 31.5 %all-to-all-start.1 = ((bf16[16,32,1024]{2,1,0:T(8,128)(2,1)}), bf16[16,32,1024]{2,1,0:T(8,128)(2,1)S(1)}, u32[]{:S(2)}, u32[]{:S(2)}) async-start(bf16[16,32,1024]{2,1,0:T(8,128)(2,1)} %bitcast.4), calls=%async_computation.1 | async-start | bytes 2097152 | tf_op jit(solution)/shard_map/all_to_all | solution.py:31
Sparse Core Ops, SparseCore 0:
  8.9 22.5 all-gather.2
  33.0 21.0 all-gather.4
where the time goes:
time: 110 us
  waiting for transfers between devices  35.4 us (32%)
  blocking collectives  34.5 us (31%)
  matrix products  15.8 us (14%)
  between operations  13.5 us (12%)
  starting transfers between devices  6.86 us (6%)
  local copies, waits for them, and re-layouts  3.09 us (3%)
    all_to_all x1, blocking collectives, on_device(): lax.all_to_all(outgoing, 'ex', split_axis=0, concat_axis=0, tiled=True)  34.5 us
    all_to_all x1, waiting for transfers between devices, on_device(): lax.all_to_all(result.astype(jnp.bfloat16).reshape(received.shape), 'ex',...  24.4 us
    dot_general x1, matrix products, on_device(): result = jnp.dot(hidden, full_out[0], preferred_element_type=jnp.float32)  15.6 us
    all_gather x1, waiting for transfers between devices, on_device(): lax.all_gather(w_out, 'grp', axis=1, tiled=True)  9.65 us
    all_to_all x1, starting transfers between devices, on_device(): lax.all_to_all(result.astype(jnp.bfloat16).reshape(received.shape), 'ex',...  6.79 us
  transfers between devices with their start and end apart: 3, of which 2 were waited for; matrix products, arithmetic and copies ran while one was open for 2% of the time, Pallas kernels for 0%

commit v1 on v0

--- a/solution.py
+++ b/solution.py
@@ -1,10 +1,263 @@
+import functools
+
 import jax
 import jax.numpy as jnp
 from jax import lax
+from jax.experimental import pallas as pl
+from jax.experimental.pallas import tpu as pltpu
 from jax.sharding import PartitionSpec as P
 
-
-def on_device(tokens, expert_ids, slot_ids, centroids, w_in, w_out):
+MESH = pl.DeviceIdType.MESH
+TILE = 512
+
+
+def expert_kernel(
+    n,
+    cap,
+    ids_ref,
+    slots_ref,
+    tokens_ref,
+    centroids_ref,
+    w_in_ref,
+    w_out_ref,
+    out_ref,
+    outgoing,
+    received,
+    result,
+    returned,
+    total,
+    place,
+    columns,
+    full_in,
+    full_out,
+    load_sem,
+    share_send,
+    share_recv,
+    send_sem,
+    recv_sem,
+    back_send,
+    back_recv,
+):
+    grp = lax.axis_index("grp")
+    me = lax.axis_index("ex")
+    half = n // 2
+    side = me // half
+    seat = me % half
+    quarter = n // 4
+    rows = quarter * cap
+    tokens_here, width = tokens_ref.shape
+    hidden = full_in.shape[2]
+
+    def peer_to(slot):
+        return ((side + slot // half) % 2) * half + (seat + slot % half) % half
+
+    def peer_from(slot):
+        return ((side + slot // half) % 2) * half + (seat + half - slot % half) % half
+
+    def block(slot):
+        start = slot * cap
+        if not isinstance(slot, int):
+            start = pl.multiple_of(start, cap)
+        return pl.ds(start, cap)
+
+    barrier = pltpu.get_barrier_semaphore()
+    for slot in range(1, n):
+        pl.semaphore_signal(
+            barrier, inc=1, device_id={"ex": peer_to(slot)}, device_id_type=MESH
+        )
+    pl.semaphore_signal(barrier, inc=1, device_id={"grp": 1 - grp}, device_id_type=MESH)
+
+    loads = [
+        pltpu.make_async_copy(w_in_ref.at[0], full_in.at[0], load_sem.at[0]),
+        pltpu.make_async_copy(w_out_ref.at[0], full_out.at[0], load_sem.at[1]),
+    ]
+    for load in loads:
+        load.start()
+
+    ids = ids_ref[...]
+    high = (ids >= half).astype(jnp.int32)
+    ahead = ids - high * half - seat
+    ahead = jnp.where(ahead < 0, ahead + half, ahead)
+    across = jnp.where(high == side, 0, 1)
+    position = (across * half + ahead) * cap + slots_ref[...]
+    slot_rows = lax.broadcasted_iota(jnp.int32, (n * cap, tokens_here), 0)
+    spread = (slot_rows == position).astype(jnp.bfloat16)
+    packed = jnp.dot(spread, tokens_ref[...], preferred_element_type=jnp.float32)
+    packed = packed.astype(jnp.bfloat16)
+    outgoing[...] = packed
+    received[block(0), :] = packed[:cap]
+
+    shares = [
+        pltpu.make_async_remote_copy(
+            src_ref=w_in_ref.at[0],
+            dst_ref=full_in.at[1],
+            send_sem=share_send.at[0],
+            recv_sem=share_recv.at[0],
+            device_id={"grp": 1 - grp},
+            device_id_type=MESH,
+        ),
+        pltpu.make_async_remote_copy(
+            src_ref=w_out_ref.at[0],
+            dst_ref=full_out.at[1],
+            send_sem=share_send.at[1],
+            recv_sem=share_recv.at[1],
+            device_id={"grp": 1 - grp},
+            device_id_type=MESH,
+        ),
+    ]
+
+    def dispatch(slot):
+        return pltpu.make_async_remote_copy(
+            src_ref=outgoing.at[block(slot), :],
+            dst_ref=received.at[block(slot), :],
+            send_sem=send_sem.at[slot],
+            recv_sem=recv_sem.at[slot],
+            device_id={"ex": peer_to(slot)},
+            device_id_type=MESH,
+        )
+
+    def give_back(slot):
+        return pltpu.make_async_remote_copy(
+            src_ref=result.at[block(slot), :],
+            dst_ref=returned.at[block(slot), :],
+            send_sem=back_send.at[slot],
+            recv_sem=back_recv.at[slot],
+            device_id={"ex": peer_from(slot)},
+            device_id_type=MESH,
+        )
+
+    pl.semaphore_wait(barrier, n)
+    for step in range(half):
+        dispatch(half + step).start()
+        if step > 0:
+            dispatch(step).start()
+    for share in shares:
+        share.start()
+
+    scores = lax.dot_general(
+        centroids_ref[...],
+        tokens_ref[...],
+        (((1,), (1,)), ((), ())),
+        preferred_element_type=jnp.float32,
+    )
+    experts = lax.broadcasted_iota(jnp.int32, scores.shape, 0)
+    chosen = jnp.sum(jnp.where(experts == ids, scores, 0.0), axis=0, keepdims=True)
+    gating = 1.0 / (1.0 + jnp.exp(-chosen))
+    lines = lax.broadcasted_iota(jnp.int32, (128, tokens_here), 0)
+    columns[...] = jnp.where(lines == 0, position.astype(jnp.float32), gating).T
+    slot_columns = lax.broadcasted_iota(jnp.int32, (tokens_here, n * cap), 1)
+    place[...] = (slot_columns == columns[:, 0:1].astype(jnp.int32)).astype(jnp.bfloat16)
+
+    for load in loads:
+        load.wait()
+    for share in shares:
+        share.wait_recv()
+
+    @pl.loop(0, 4)
+    def _(turn):
+        chunk = (2 + 2 * turn) % 4 + turn // 2
+        first = chunk * quarter
+
+        @pl.loop(0, quarter)
+        def _(k):
+            @pl.when(first + k > 0)
+            def _():
+                dispatch(first + k).wait_recv()
+
+        here = pl.ds(pl.multiple_of(chunk * rows, rows), rows)
+        total[...] = jnp.zeros_like(total)
+
+        @pl.loop(0, 2 * (hidden // TILE))
+        def _(piece):
+            part = piece // (hidden // TILE)
+            cut = pl.ds(pl.multiple_of((piece % (hidden // TILE)) * TILE, TILE), TILE)
+            middle = jnp.dot(
+                received[here, :], full_in[part, :, cut], preferred_element_type=jnp.float32
+            )
+            middle = jnp.maximum(middle, 0.0).astype(jnp.bfloat16)
+            total[...] += jnp.dot(
+                middle, full_out[part, cut, :], preferred_element_type=jnp.float32
+            )
+
+        result[here, :] = total[...].astype(jnp.bfloat16)
+
+        @pl.loop(0, quarter)
+        def _(k):
+            @pl.when(first + k > 0)
+            def _():
+                give_back(first + k).start()
+
+            @pl.when(first + k == 0)
+            def _():
+                returned[block(0), :] = result[block(0), :]
+
+    arrived = jnp.zeros((tokens_here, width), jnp.float32)
+    for chunk in range(4):
+        for slot in range(chunk * quarter, (chunk + 1) * quarter):
+            if slot > 0:
+                give_back(slot).wait_recv()
+        here = pl.ds(chunk * rows, rows)
+        arrived += jnp.dot(
+            place[:, here], returned[here, :], preferred_element_type=jnp.float32
+        )
+    mixed = tokens_ref[...].astype(jnp.float32) + columns[:, 1:2] * arrived
+    out_ref[...] = mixed.astype(jnp.bfloat16)
+
+    @pl.loop(1, n)
+    def _(slot):
+        dispatch(slot).wait_send()
+        give_back(slot).wait_send()
+
+    for share in shares:
+        share.wait_send()
+
+
+def in_one_kernel(n, tokens, expert_ids, slot_ids, centroids, w_in, w_out):
+    count, width = tokens.shape
+    cap = 2 * count // n
+    slots = n * cap
+    rows = slots // 4
+    hidden = w_in.shape[2]
+    vmem = pl.BlockSpec(memory_space=pltpu.VMEM)
+    hbm = pl.BlockSpec(memory_space=pl.ANY)
+    sems = pltpu.SemaphoreType.DMA
+    return pl.pallas_call(
+        functools.partial(expert_kernel, n, cap),
+        out_shape=jax.ShapeDtypeStruct((count, width), jnp.bfloat16),
+        in_specs=[vmem, vmem, vmem, vmem, hbm, hbm],
+        out_specs=vmem,
+        scratch_shapes=[
+            pltpu.VMEM((slots, width), jnp.bfloat16),
+            pltpu.VMEM((slots, width), jnp.bfloat16),
+            pltpu.VMEM((slots, width), jnp.bfloat16),
+            pltpu.VMEM((slots, width), jnp.bfloat16),
+            pltpu.VMEM((rows, width), jnp.float32),
+            pltpu.VMEM((count, slots), jnp.bfloat16),
+            pltpu.VMEM((count, 128), jnp.float32),
+            pltpu.VMEM((2, width, hidden), jnp.bfloat16),
+            pltpu.VMEM((2, hidden, width), jnp.bfloat16),
+            sems((2,)),
+            sems((2,)),
+            sems((2,)),
+            sems((n,)),
+            sems((n,)),
+            sems((n,)),
+            sems((n,)),
+        ],
+        compiler_params=pltpu.CompilerParams(
+            collective_id=0, has_side_effects=True, vmem_limit_bytes=60 * 1024 * 1024
+        ),
+    )(
+        expert_ids.reshape(1, count),
+        slot_ids.reshape(1, count),
+        tokens,
+        centroids,
+        w_in,
+        w_out,
+    )
+
+
+def in_plain_ops(tokens, expert_ids, slot_ids, centroids, w_in, w_out):
     experts = centroids.shape[0]
     count_rows = tokens.shape[0]
     model_width = tokens.shape[1]
@@ -41,6 +294,14 @@
 
 
 def solution(mesh):
+    n = mesh.shape["ex"]
+
+    def on_device(tokens, expert_ids, slot_ids, centroids, w_in, w_out):
+        capacity = 2 * tokens.shape[0] // n
+        if mesh.shape["grp"] == 2 and n % 4 == 0 and capacity % 16 == 0:
+            return in_one_kernel(n, tokens, expert_ids, slot_ids, centroids, w_in, w_out)
+        return in_plain_ops(tokens, expert_ids, slot_ids, centroids, w_in, w_out)
+
     in_specs = (
         P(("grp", "ex"), None),
         P(("grp", "ex")),

time: 110 us -> 60.6 us (0.55)
  Pallas kernels: 0 us -> 58.6 us
  waiting for transfers between devices: 35.4 us -> 0 us
  blocking collectives: 34.5 us -> 0 us
  matrix products: 15.8 us -> 0 us
  between operations: 13.5 us -> 0.01 us
  starting transfers between devices: 6.86 us -> 0 us
  local copies, waits for them, and re-layouts: 3.09 us -> 1.87 us
    pallas_call x0 -> x1, Pallas kernels: none -> 58.6 us  [in_one_kernel(): pl.pallas_call(functools.partial(expert_kernel, n, cap), out_shape=jax.Sh...]
    all_to_all x1 -> x0, blocking collectives: 34.5 us -> none  [on_device(): lax.all_to_all(outgoing, 'ex', split_axis=0, concat_axis=0, tiled=True)]
    all_to_all x1 -> x0, waiting for transfers between devices: 24.4 us -> none  [on_device(): lax.all_to_all(result.astype(jnp.bfloat16).reshape(received.shape), 'ex',...]
    dot_general x2 -> x0, matrix products: 15.8 us -> none  [the longest x1 15.6 us: on_device(): result = jnp.dot(hidden, full_out[0], preferred_element_type=jnp.float32)]
    all_gather x2 -> x0, waiting for transfers between devices: 9.65 us -> none  [the longest x1 9.65 us: on_device(): lax.all_gather(w_out, 'grp', axis=1, tiled=True)]
    all_to_all x1 -> x0, starting transfers between devices: 6.79 us -> none  [on_device(): lax.all_to_all(result.astype(jnp.bfloat16).reshape(received.shape), 'ex',...]
    scatter x1 -> x0, local copies, waits for them, and re-layouts: 1.91 us -> none  [on_device(): jnp.zeros((experts * capacity, model_width), jnp.bfloat16).at[buffer_rows]]
    unnamed x8 -> x1, local copies, waits for them, and re-layouts: 0.02 us -> 1.87 us
  transfers between devices with their start and end apart: 3 -> 0, of which waited for: 2 -> 0; matrix products, arithmetic and copies ran while one was open for 2% -> 0% of each run, Pallas kernels for 0% -> 0%
where the time goes in v1:
time: 60.6 us; the launch traced here: 60.5 us
  Pallas kernels  58.6 us (97%)
  local copies, waits for them, and re-layouts  1.87 us (3%)
    pallas_call x1, Pallas kernels, in_one_kernel(): pl.pallas_call(functools.partial(expert_kernel, n, cap), out_shape=jax.Sh...  58.6 us
    unnamed x1, local copies, waits for them, and re-layouts  1.87 us

profile of v1, /device:TPU:0, one launch (start us, length us, event | category | flops | bytes accessed | tf_op | source)
XLA Modules:
  0.0 60.5 jit_solution(6182096450254608137)
XLA Ops:
  0.0 58.6 %shard_map.64 = bf16[256,1024]{1,0:T(8,128)(2,1)} custom-call(s32[1,256]{1,0:T(1,128)} %bitcast.2, s32[1,256]{1,0:T(1,128)} %bitcast.3, bf16[256,1024]{1,0:T(8,128)(2,1)} %tokens_ref.1, bf16[16,1024]{1,0:T(8,128)(2,1)} %centroids_ref.1, bf16[1,1024,2048]{2,1,0:T(8,128)(2,1)} %w_in_ref.1, bf16[1,2048,1024]{2,1,0:T(8,128)(2,1)} %w_out_ref.1), custom_call_target="tpu_custom_call" | custom-call | tf_op jit(solution)/shard_map/pallas_call | solution.py:224
  58.6 1.9 %copy.8 = bf16[256,1024]{1,0:T(8,128)(2,1)} copy(bf16[256,1024]{1,0:T(8,128)(2,1)} %shard_map.64) | data formatting | bytes 1048576

commit v2 on v1

--- a/solution.py
+++ b/solution.py
@@ -8,7 +8,7 @@
 from jax.sharding import PartitionSpec as P
 
 MESH = pl.DeviceIdType.MESH
-TILE = 512
+TILE = 1024
 
 
 def expert_kernel(
@@ -127,7 +127,7 @@
         )
 
     pl.semaphore_wait(barrier, n)
-    for step in range(half):
+    for step in reversed(range(half)):
         dispatch(half + step).start()
         if step > 0:
             dispatch(step).start()
@@ -155,7 +155,7 @@
 
     @pl.loop(0, 4)
     def _(turn):
-        chunk = (2 + 2 * turn) % 4 + turn // 2
+        chunk = 3 - (2 * turn) % 4 - turn // 2
         first = chunk * quarter
 
         @pl.loop(0, quarter)
@@ -192,7 +192,7 @@
                 returned[block(0), :] = result[block(0), :]
 
     arrived = jnp.zeros((tokens_here, width), jnp.float32)
-    for chunk in range(4):
+    for chunk in (1, 3, 0, 2):
         for slot in range(chunk * quarter, (chunk + 1) * quarter):
             if slot > 0:
                 give_back(slot).wait_recv()

time: 60.6 us -> 57.9 us (0.955)
  Pallas kernels: 58.6 us -> 55.9 us
    pallas_call x1, Pallas kernels: 58.6 us -> 55.9 us  [in_one_kernel(): pl.pallas_call(functools.partial(expert_kernel, n, cap), out_shape=jax.Sh...]
where the time goes in v2:
time: 57.9 us; the launch traced here: 57.7 us
  Pallas kernels  55.9 us (97%)
  local copies, waits for them, and re-layouts  1.87 us (3%)
    pallas_call x1, Pallas kernels, in_one_kernel(): pl.pallas_call(functools.partial(expert_kernel, n, cap), out_shape=jax.Sh...  55.9 us
    unnamed x1, local copies, waits for them, and re-layouts  1.87 us

profile of v2, /device:TPU:0, one launch (start us, length us, event | category | flops | bytes accessed | tf_op | source)
XLA Modules:
  0.0 57.7 jit_solution(9980500495751143804)
XLA Ops:
  0.0 55.9 %shard_map.64 = bf16[256,1024]{1,0:T(8,128)(2,1)} custom-call(s32[1,256]{1,0:T(1,128)} %bitcast.2, s32[1,256]{1,0:T(1,128)} %bitcast.3, bf16[256,1024]{1,0:T(8,128)(2,1)} %tokens_ref.1, bf16[16,1024]{1,0:T(8,128)(2,1)} %centroids_ref.1, bf16[1,1024,2048]{2,1,0:T(8,128)(2,1)} %w_in_ref.1, bf16[1,2048,1024]{2,1,0:T(8,128)(2,1)} %w_out_ref.1), custom_call_target="tpu_custom_call" | custom-call | tf_op jit(solution)/shard_map/pallas_call | solution.py:224
  55.9 1.9 %copy.8 = bf16[256,1024]{1,0:T(8,128)(2,1)} copy(bf16[256,1024]{1,0:T(8,128)(2,1)} %shard_map.64) | data formatting | bytes 1048576

commit v3 on v2

--- a/solution.py
+++ b/solution.py
@@ -16,7 +16,7 @@
     cap,
     ids_ref,
     slots_ref,
-    tokens_ref,
+    tokens_hbm,
     centroids_ref,
     w_in_ref,
     w_out_ref,
@@ -26,6 +26,7 @@
     result,
     returned,
     total,
+    tokens_ref,
     place,
     columns,
     full_in,
@@ -67,6 +68,8 @@
         )
     pl.semaphore_signal(barrier, inc=1, device_id={"grp": 1 - grp}, device_id_type=MESH)
 
+    bring = pltpu.make_async_copy(tokens_hbm, tokens_ref, load_sem.at[2])
+    bring.start()
     loads = [
         pltpu.make_async_copy(w_in_ref.at[0], full_in.at[0], load_sem.at[0]),
         pltpu.make_async_copy(w_out_ref.at[0], full_out.at[0], load_sem.at[1]),
@@ -82,6 +85,7 @@
     position = (across * half + ahead) * cap + slots_ref[...]
     slot_rows = lax.broadcasted_iota(jnp.int32, (n * cap, tokens_here), 0)
     spread = (slot_rows == position).astype(jnp.bfloat16)
+    bring.wait()
     packed = jnp.dot(spread, tokens_ref[...], preferred_element_type=jnp.float32)
     packed = packed.astype(jnp.bfloat16)
     outgoing[...] = packed
@@ -223,8 +227,8 @@
     sems = pltpu.SemaphoreType.DMA
     return pl.pallas_call(
         functools.partial(expert_kernel, n, cap),
-        out_shape=jax.ShapeDtypeStruct((count, width), jnp.bfloat16),
-        in_specs=[vmem, vmem, vmem, vmem, hbm, hbm],
+        out_shape=pltpu.VMEM((count, width), jnp.bfloat16),
+        in_specs=[vmem, vmem, hbm, vmem, hbm, hbm],
         out_specs=vmem,
         scratch_shapes=[
             pltpu.VMEM((slots, width), jnp.bfloat16),
@@ -232,11 +236,12 @@
             pltpu.VMEM((slots, width), jnp.bfloat16),
             pltpu.VMEM((slots, width), jnp.bfloat16),
             pltpu.VMEM((rows, width), jnp.float32),
+            pltpu.VMEM((count, width), jnp.bfloat16),
             pltpu.VMEM((count, slots), jnp.bfloat16),
             pltpu.VMEM((count, 128), jnp.float32),
             pltpu.VMEM((2, width, hidden), jnp.bfloat16),
             pltpu.VMEM((2, hidden, width), jnp.bfloat16),
-            sems((2,)),
+            sems((3,)),
             sems((2,)),
             sems((2,)),
             sems((n,)),

time: 57.9 us -> 56.1 us (0.969)
  local copies, waits for them, and re-layouts: 1.87 us -> 0.8 us
  Pallas kernels: 55.9 us -> 55.1 us
    unnamed x1, local copies, waits for them, and re-layouts: 1.87 us -> 0.8 us
    pallas_call x1, Pallas kernels: 55.9 us -> 55.1 us  [in_one_kernel(): pl.pallas_call(functools.partial(expert_kernel, n, cap), out_shape=pltpu....]
where the time goes in v3:
time: 56.1 us; the launch traced here: 55.9 us
  Pallas kernels  55.1 us (98%)
  local copies, waits for them, and re-layouts  0.8 us (1%)
    pallas_call x1, Pallas kernels, in_one_kernel(): pl.pallas_call(functools.partial(expert_kernel, n, cap), out_shape=pltpu....  55.1 us

profile of v3, /device:TPU:0, one launch (start us, length us, event | category | flops | bytes accessed | tf_op | source)
XLA Modules:
  0.0 55.9 jit_solution(4677579809490418733)
XLA Ops:
  0.0 55.1 %shard_map.64 = bf16[256,1024]{1,0:T(8,128)(2,1)S(1)} custom-call(s32[1,256]{1,0:T(1,128)} %bitcast.2, s32[1,256]{1,0:T(1,128)} %bitcast.3, bf16[256,1024]{1,0:T(8,128)(2,1)} %tokens_hbm.1, bf16[16,1024]{1,0:T(8,128)(2,1)} %centroids_ref.1, bf16[1,1024,2048]{2,1,0:T(8,128)(2,1)} %w_in_ref.1, bf16[1,2048,1024]{2,1,0:T(8,128)(2,1)} %w_out_ref.1), custom_call_target="tpu_custom_call" | custom-call | tf_op jit(solution)/shard_map/pallas_call | solution.py:228
  55.1 0.8 %copy.8 = bf16[256,1024]{1,0:T(8,128)(2,1)} copy(bf16[256,1024]{1,0:T(8,128)(2,1)S(1)} %shard_map.64) | data formatting | bytes 1048576
